TPU v7x, 32 devices: a whole 2x2x4 slice. The times are simulated.
32 devices in a mesh: dp: 8 (over y, x, core), seq: 4 (over z).
Axes of the slice: x: 2, y: 2, z: 4, core: 2. Of those that a mesh axis runs over, the one named last changes fastest.
Arguments:
- queries: bfloat16 [8, 1024, 2048], P('dp', 'seq'), may hold values from -6 to 6
- keys: bfloat16 [8, 1024, 1024], P('dp', 'seq'), may hold values from -6 to 6
- values: bfloat16 [8, 1024, 1024], P('dp', 'seq'), may hold values from -190 to 190
- segments: int32 [8, 1024], P('dp', 'seq'), may hold values from 0 to 2, never falling along the last dimension, each value on 1 to 640 neighbouring positions
- cotangent: bfloat16 [8, 1024, 2304], P('dp', 'seq'), may hold values from -6 to 6
- weight: float32 [2048, 2304], P(('dp', 'seq')), may hold values from -0.125 to 0.125
- first_moment: bfloat16 [2048, 2304], P(('dp', 'seq')), may hold values from -1 to 1
- first_scale: float32 [2048, 18], P(('dp', 'seq')), may hold values from 0.3 to 3
- second_moment: bfloat16 [2048, 2304], P(('dp', 'seq')), may hold values from 0.049804688 to 1
- second_scale: float32 [2048, 18], P(('dp', 'seq')), may hold values from 0.3 to 3
Outputs:
- layer_out: bfloat16 [8, 1024, 2304], P('dp', 'seq')
- new_weight: float32 [2048, 2304], P(('dp', 'seq'))
- new_first: bfloat16 [2048, 2304], P(('dp', 'seq'))
- new_first_scale: float32 [2048, 18], P(('dp', 'seq'))
- new_second: bfloat16 [2048, 2304], P(('dp', 'seq'))
- new_second_scale: float32 [2048, 18], P(('dp', 'seq'))
Inputs may be any that keep to these rules, and one draw needn't show every extreme that they name: `segments`: document numbers never fall along a sequence; each sequence holds 3 documents, one of exactly 640 positions.
All inputs are finite; a program needn't handle non-finite values. Where the computation divides by a largest or mean magnitude, that divisor is 1e-20 or more.
Results may differ from a plain program's by a relative error of at most 0.01.
Values may be sent and summed in bfloat16 or wider, within the bound.
A program may use at most 128 MiB of HBM per device.

v0:
```python
import jax
import jax.numpy as jnp
from jax import lax
from jax.sharding import PartitionSpec as P

HEADS = 16
KV_HEADS = 8
HEAD_DIM = 128
DO = 2304
GROUP = 128
QW = 2048


score_scale = 144.0 ** (-0.5)
soft_cap = 50.0
beta_first = 0.9
beta_second = 0.95
learn_rate = 0.001
decay_rate = 0.1


def quantize(blocks):
    grouped = blocks.astype(jnp.float32).reshape(blocks.shape[0], KV_HEADS, HEAD_DIM)
    scales = (jnp.max(jnp.abs(grouped), axis=-1) + 1e-06).astype(jnp.bfloat16)
    coded = (grouped / scales.astype(jnp.float32)[..., None]).astype(jnp.bfloat16)
    return (coded, scales)


def recover_values(coded, scales):
    return (coded.astype(jnp.float32) * scales.astype(jnp.float32)[..., None]).astype(jnp.bfloat16)


def decode(coded, scales):
    values_f = coded.astype(jnp.float32).reshape(coded.shape[0], -1, GROUP)
    return (scales[..., None] * jnp.sign(values_f) * jnp.sqrt(jnp.abs(values_f))).reshape(
        coded.shape
    )


def encode(moment):
    grouped = moment.reshape(moment.shape[0], -1, GROUP)
    scales = jnp.max(jnp.abs(grouped), axis=-1) + 1e-06
    coded = (grouped * jnp.abs(grouped) / (scales[..., None] * scales[..., None])).astype(
        jnp.bfloat16
    )
    return (coded.reshape(moment.shape), scales)


def local(
    queries,
    keys,
    values,
    segments,
    cotangent,
    weight,
    first_moment,
    first_scale,
    second_moment,
    second_scale,
):
    query_rows = queries[0]
    tokens_here = query_rows.shape[0]
    repeat_heads = HEADS // KV_HEADS
    grouped_queries = query_rows.reshape(tokens_here, KV_HEADS, repeat_heads, HEAD_DIM)
    positions = lax.axis_index("seq") * tokens_here + jnp.arange(tokens_here, dtype=jnp.int32)
    own_docs = segments[0]
    key_codes, key_scale_factors = quantize(keys[0])
    value_codes, value_scale_factors = quantize(values[0])
    portion_keys = lax.all_gather(key_codes, "seq", axis=0, tiled=True)
    portion_key_scale = lax.all_gather(key_scale_factors, "seq", axis=0, tiled=True)
    piece_values = lax.all_gather(value_codes, "seq", axis=0, tiled=True)
    piece_vscale = lax.all_gather(value_scale_factors, "seq", axis=0, tiled=True)
    piece_docs = lax.all_gather(own_docs, "seq", axis=0, tiled=True)
    count_rows = portion_keys.shape[0]
    key_estimate = recover_values(portion_keys, portion_key_scale)
    value_hat = recover_values(piece_values, piece_vscale)
    scores = (
        jnp.einsum(
            "qgrd,kgd->qgrk", grouped_queries, key_estimate, preferred_element_type=jnp.float32
        )
        * score_scale
    )
    capped = soft_cap * jnp.tanh(scores / soft_cap)
    key_places = jnp.arange(count_rows, dtype=jnp.int32)
    allowed = (own_docs[:, None] == piece_docs[None, :]) & (
        key_places[None, :] <= positions[:, None]
    )
    weights = jnp.where(allowed[:, None, None, :], jnp.exp(capped), jnp.float32(0.0))
    denom = jnp.sum(weights, axis=-1)
    numer = jnp.einsum(
        "qgrk,kgd->qgrd",
        weights.astype(jnp.bfloat16),
        value_hat,
        preferred_element_type=jnp.float32,
    )
    numer, denom = (numer, denom)
    attended = (
        (numer / denom[..., None]).reshape(tokens_here, HEADS * HEAD_DIM).astype(jnp.bfloat16)
    )
    weight_low = weight.astype(jnp.bfloat16)
    columns = attended
    projected = jnp.dot(
        columns,
        lax.all_gather(weight_low, ("dp", "seq"), axis=0, tiled=True),
        preferred_element_type=jnp.float32,
    )
    layer_out = projected.astype(jnp.bfloat16)[None]
    cot_rows = cotangent[0]
    columns = attended
    group_sum = lax.psum_scatter(
        lax.dot_general(
            columns, cot_rows, (((0,), (0,)), ((), ())), preferred_element_type=jnp.float32
        ).astype(jnp.bfloat16),
        "dp",
        scatter_dimension=0,
        tiled=True,
    )
    gradient_matrix = lax.psum_scatter(group_sum, "seq", scatter_dimension=0, tiled=True).astype(
        jnp.float32
    )
    sum_squares = lax.psum(jnp.sum(gradient_matrix * gradient_matrix), ("dp", "seq"))
    rms_value = jnp.sqrt(sum_squares / (QW * DO) + 1e-06)
    clipped = gradient_matrix * jnp.minimum(jnp.float32(1.0), 1.0 / rms_value)
    first = beta_first * decode(first_moment, first_scale) + (1.0 - beta_first) * clipped
    second = (
        beta_second * decode(second_moment, second_scale) + (1.0 - beta_second) * clipped * clipped
    )
    new_weight = weight - learn_rate * (first / (jnp.sqrt(second) + 1e-08) + decay_rate * weight)
    new_first, new_first_scale = encode(first)
    new_second, new_second_scale = encode(second)
    return (layer_out, new_weight, new_first, new_first_scale, new_second, new_second_scale)


def solution(mesh):
    return jax.shard_map(
        local,
        mesh=mesh,
        in_specs=(
            P("dp", "seq", None),
            P("dp", "seq", None),
            P("dp", "seq", None),
            P("dp", "seq"),
            P("dp", "seq", None),
            P(("dp", "seq"), None),
            P(("dp", "seq"), None),
            P(("dp", "seq"), None),
            P(("dp", "seq"), None),
            P(("dp", "seq"), None),
        ),
        out_specs=(
            P("dp", "seq", None),
            P(("dp", "seq"), None),
            P(("dp", "seq"), None),
            P(("dp", "seq"), None),
            P(("dp", "seq"), None),
            P(("dp", "seq"), None),
        ),
        check_vma=False,
    )
```

profile of v0, /device:TPU:0, one launch (start us, length us, event | category | flops | bytes accessed | tf_op | source)
XLA Modules:
  0.0 381.8 jit_solution(442166706942635452)
XLA Ops:
  7.2 0.0 copy-start
  7.2 0.0 copy-start.3
  7.2 0.0 all-gather.7.cloned.1.call-start
  7.2 1.3 convert_bitcast_fusion
  8.5 0.2 copy.56
  8.7 0.3 abs_reduce_fusion
  9.1 1.1 divide_convert_fusion
  10.2 0.0 all-gather.7.cloned.1.call-update
  10.3 0.0 copy-start.1
  10.3 0.0 all-gather.5.cloned.1.call-start
  10.3 0.0 copy-done.3
  10.3 0.1 convert_bitcast_fusion.1
  10.4 0.2 copy.55
  10.7 0.0 copy-start.8
  10.7 0.3 abs_reduce_fusion.1
  11.0 1.1 divide_convert_fusion.1
  12.2 0.0 all-gather.5.cloned.1.call-update
  12.2 0.0 reduce-scatter.3.cloned.1.call-start
  12.3 17.1 %all_gather.22 = bf16[1024,8]{1,0:T(8,128)(2,1)S(1)} all-gather(bf16[256,8]{1,0:T(8,128)(2,1)S(1)} %get-tuple-element.25), channel_id=1, replica_groups=mesh['dp'=8,'seq'=4] {'seq'}, dimensions={0}, use_global_device_ids=true | all-gather | bytes 20480 | tf_op jit(solution)/shard_map/all_gather | solution.py:70
  29.4 0.0 copy-done.1
  29.4 1.5 reshape_squeeze.3
  31.0 0.0 copy-start.2
  31.0 17.3 %all_gather.19 = bf16[1024,8]{1,0:T(8,128)(2,1)S(1)} all-gather(bf16[256,8]{1,0:T(8,128)(2,1)S(1)} %get-tuple-element.23), channel_id=1, replica_groups=mesh['dp'=8,'seq'=4] {'seq'}, dimensions={0}, use_global_device_ids=true | all-gather | bytes 20480 | tf_op jit(solution)/shard_map/all_gather | solution.py:72
  48.3 0.0 copy-done.8
  48.4 11.5 %all-gather = s32[1,1024]{1,0:T(1,128)S(1)} all-gather(s32[1,256]{1,0:T(1,128)S(1)} %copy-done.8), channel_id=2, replica_groups=mesh['dp'=8,'seq'=4] {'seq'}, dimensions={1}, use_global_device_ids=true | all-gather | bytes 5120 | tf_op jit(solution)/shard_map/all_gather | solution.py:73
  59.8 0.3 fusion.14
  60.1 4.7 %all-gather.7.cloned.1.call-done = bf16[1024,8,128]{2,1,0:T(8,128)(2,1)} async-done(((bf16[256,8,128]{2,1,0:T(8,128)(2,1)}), bf16[1024,8,128]{2,1,0:T(8,128)(2,1)}) %all-gather.7.cloned.1.call-update) | async-done | bytes 2097168 | tf_op jit(solution)/shard_map/all_gather | solution.py:69
  64.8 2.5 fusion.7
  67.2 0.0 copy-done.2
  67.3 8.6 %fusion = (f32[256,8,2]{0,2,1:T(2,128)S(1)}, f32[8,1024,256,2]{2,1,3,0:T(8,128)}) fusion(pred[256,1024]{0,1:T(8,128)(4,1)S(1)} %fusion.14, bf16[256,8,2,128]{3,2,1,0:T(2,128)(2,1)S(1)} %copy-done.2, bf16[1024,8,128,1]{2,1,0,3:T(8,128)(2,1)S(1)} %fusion.7), kind=kOutput, calls=%fused_computation.1 | convolution fusion | flops 1090514944 | bytes 20201472 | tf_op jit(solution)/shard_map/qgrd,kgd->qgrk/dot_general | solution.py:78
  75.9 35.2 %all-gather.5.cloned.1.call-done = bf16[1024,8,128]{2,1,0:T(8,128)(2,1)} async-done(((bf16[256,8,128]{2,1,0:T(8,128)(2,1)}), bf16[1024,8,128]{2,1,0:T(8,128)(2,1)}) %all-gather.5.cloned.1.call-update) | async-done | bytes 2097168 | tf_op jit(solution)/shard_map/all_gather | solution.py:71
  111.1 2.5 fusion.6
  113.6 8.7 %fusion.8 = bf16[256,8,2,128]{0,3,2,1:T(8,128)(2,1)S(1)} fusion(f32[256,8,2]{0,2,1:T(2,128)S(1)} %get-tuple-element.36, f32[8,1024,256,2]{2,1,3,0:T(8,128)} %get-tuple-element.37, pred[256,1024]{0,1:T(8,128)(4,1)S(1)} %fusion.14, bf16[1024,8,128,1]{2,1,0,3:T(8,128)(2,1)S(1)} %fusion.6), kind=kOutput, calls=%fused_computation.13 | convolution fusion | flops 1091567616 | bytes 20201472 | tf_op jit(solution)/shard_map/qgrk,kgd->qgrd/dot_general | solution.py:90
  122.3 0.0 copy-done
  122.3 5.0 %convolution_convert_fusion = bf16[2048,2304]{1,0:T(8,128)(2,1)} fusion(bf16[256,2048]{0,1:T(8,128)(2,1)S(1)} %bitcast.58, bf16[1,256,2304]{2,1,0:T(8,128)(2,1)S(1)} %copy-done), kind=kOutput, calls=%fused_computation.3 | convolution fusion | flops 2420637696 | bytes 11665408 | tf_op jit(solution)/shard_map/dot_general | solution.py:111
  127.3 0.0 reduce-scatter.3.cloned.1.call-update
  127.3 0.0 reduce-scatter.5.cloned.1.call-start
  127.4 75.7 %reduce-scatter.3.cloned.1.call-done = bf16[256,2304]{1,0:T(8,128)(2,1)} async-done(((bf16[2048,2304]{1,0:T(8,128)(2,1)}), bf16[256,2304]{1,0:T(8,128)(2,1)}) %reduce-scatter.3.cloned.1.call-update) | async-done | bytes 1179664 | tf_op jit(solution)/shard_map/reduce_scatter | solution.py:110
  203.1 0.0 reduce-scatter.5.cloned.1.call-update
  203.1 0.0 all-gather.9.cloned.1.call-start
  203.2 0.0 copy-done.6
  203.2 0.1 copy.44
  203.3 31.4 %reduce-scatter.5.cloned.1.call-done = bf16[64,2304]{1,0:T(8,128)(2,1)} async-done(((bf16[256,2304]{1,0:T(8,128)(2,1)}), bf16[64,2304]{1,0:T(8,128)(2,1)}) %reduce-scatter.5.cloned.1.call-update) | async-done | bytes 294928 | tf_op jit(solution)/shard_map/reduce_scatter | solution.py:118
  234.6 1.7 fusion.25
  236.4 0.0 copy-done.7
  236.4 0.1 copy.45
  236.4 39.2 %psum.7 = f32[]{:T(128)} all-reduce(f32[]{:T(128)} %fusion.25), channel_id=1, replica_groups=mesh['dp'=8,'seq'=4] {'dp','seq'}, use_global_device_ids=true, to_apply=%region_6.7 | all-reduce | flops 1 | bytes 8 | tf_op jit(solution)/shard_map/psum | solution.py:121
  276.3 0.3 mul.127
  276.6 0.3 mul.137
  276.8 0.0 copy-done.4
  276.9 0.0 copy-done.5
  276.9 2.9 fusion.38
  279.8 1.1 abs.43
  281.0 0.3 reduce_max.38
  281.2 1.2 abs.45
  282.4 0.3 reduce_max.39
  282.7 0.3 div.68
  283.0 0.3 div.71
  283.2 3.1 fusion.31
  286.3 0.0 all-gather.9.cloned.1.call-update
  286.4 0.7 copy.46
  287.0 0.7 copy.47
  287.7 80.2 %all-gather.9.cloned.1.call-done = bf16[2048,2304]{1,0:T(8,128)(2,1)} async-done(((bf16[64,2304]{1,0:T(8,128)(2,1)}), bf16[2048,2304]{1,0:T(8,128)(2,1)}) %all-gather.9.cloned.1.call-update) | async-done | bytes 9437200 | tf_op jit(solution)/shard_map/all_gather | solution.py:104
  368.0 7.3 %fusion.5 = bf16[1,256,2304]{2,1,0:T(8,128)(2,1)} fusion(bf16[256,2048]{0,1:T(8,128)(2,1)S(1)} %bitcast.59, bf16[2048,2304]{1,0:T(8,128)(2,1)} %all-gather.9.cloned.1.call-done), kind=kOutput, calls=%fused_computation.9 | convolution fusion | flops 2416508928 | bytes 11665408 | tf_op jit(solution)/shard_map/dot_general | solution.py:102
  (11 shorter events, 0.1 us)
Async XLA Ops:
  7.2 115.1 %copy-start = (bf16[1,256,2304]{2,1,0:T(8,128)(2,1)S(1)}, bf16[1,256,2304]{2,1,0:T(8,128)(2,1)}, u32[]{:S(2)}) copy-start(bf16[1,256,2304]{2,1,0:T(8,128)(2,1)} %param.14) | copy-start | bytes 3538948
  7.2 3.1 copy-start.3
  7.2 57.6 %all-gather.7.cloned.1.call-start = ((), (), s32[]{:S(2)}) async-start(), calls=%async_computation.3 | async-start | bytes 2621440 | tf_op jit(solution)/shard_map/all_gather | solution.py:69
  10.3 19.1 %copy-start.1 = (bf16[1,256,2048]{2,1,0:T(8,128)(2,1)S(1)}, bf16[1,256,2048]{2,1,0:T(8,128)(2,1)}, u32[]{:S(2)}) copy-start(bf16[1,256,2048]{2,1,0:T(8,128)(2,1)} %param.10) | copy-start | bytes 3145732
  10.3 100.8 %all-gather.5.cloned.1.call-start = ((), (), s32[]{:S(2)}) async-start(), calls=%async_computation.2 | async-start | bytes 2621440 | tf_op jit(solution)/shard_map/all_gather | solution.py:71
  10.7 37.7 %copy-start.8 = (s32[1,256]{1,0:T(1,128)S(1)}, s32[1,256]{1,0:T(1,128)}, u32[]{:S(2)}) copy-start(s32[1,256]{1,0:T(1,128)} %param.13) | copy-start | bytes 3076
  12.2 190.9 %reduce-scatter.3.cloned.1.call-start = ((), (), s32[]{:S(2)}) async-start(), calls=%async_computation.5 | async-start | bytes 10616832 | tf_op jit(solution)/shard_map/reduce_scatter | solution.py:110
  31.0 36.3 %copy-start.2 = (bf16[256,8,2,128]{3,2,1,0:T(2,128)(2,1)S(1)}, bf16[256,8,2,128]{3,2,1,0:T(2,128)(2,1)}, u32[]{:S(2)}) copy-start(bf16[256,8,2,128]{3,2,1,0:T(2,128)(2,1)} %reshape_squeeze.3) | copy-start | bytes 3145732
  127.3 75.9 %copy-start.6 = (f32[64,18]{0,1:T(8,128)S(1)}, f32[64,18]{0,1:T(8,128)}, u32[]{:S(2)}) copy-start(f32[64,18]{0,1:T(8,128)} %param.17) | copy-start | bytes 13828
  127.3 109.0 %copy-start.7 = (f32[64,18]{0,1:T(8,128)S(1)}, f32[64,18]{0,1:T(8,128)}, u32[]{:S(2)}) copy-start(f32[64,18]{0,1:T(8,128)} %param.19) | copy-start | bytes 13828
  127.3 149.5 %copy-start.4 = (bf16[64,2304]{1,0:T(8,128)(2,1)S(1)}, bf16[64,2304]{1,0:T(8,128)(2,1)}, u32[]{:S(2)}) copy-start(bf16[64,2304]{1,0:T(8,128)(2,1)} %param.18) | copy-start | bytes 884740
  127.3 149.5 %copy-start.5 = (bf16[64,2304]{1,0:T(8,128)(2,1)S(1)}, bf16[64,2304]{1,0:T(8,128)(2,1)}, u32[]{:S(2)}) copy-start(bf16[64,2304]{1,0:T(8,128)(2,1)} %param.16) | copy-start | bytes 884740
  127.3 107.3 %reduce-scatter.5.cloned.1.call-start = ((), (), s32[]{:S(2)}) async-start(), calls=%async_computation.6 | async-start | bytes 1474560 | tf_op jit(solution)/shard_map/reduce_scatter | solution.py:118
  203.1 164.8 %all-gather.9.cloned.1.call-start = ((), (), s32[]{:S(2)}) async-start(), calls=%async_computation.4 | async-start | bytes 9732096 | tf_op jit(solution)/shard_map/all_gather | solution.py:104
Sparse Core Ops, SparseCore 0:
  10.4 54.3 all-gather.6
  66.3 44.6 all-gather.4
  127.5 75.5 reduce-scatter.2
  205.3 29.3 reduce-scatter.4
  286.5 81.4 all-gather.8
where the time goes:
time: 382 us
  waiting for transfers between devices  227 us (59%)
  blocking collectives  85.1 us (22%)
  matrix products  29.7 us (8%)
  other arithmetic  17.9 us (5%)
  between operations  14.7 us (4%)
  local copies, waits for them, and re-layouts  6.89 us (2%)
    all_gather x1, waiting for transfers between devices, local(): lax.all_gather(weight_low, ('dp', 'seq'), axis=0, tiled=True)  80.2 us
    reduce_scatter x1, waiting for transfers between devices, local(): lax.psum_scatter(lax.dot_general(columns, cot_rows, (((0,), (0,)), ((), (...  75.7 us
    psum x1, blocking collectives, local(): lax.psum(jnp.sum(gradient_matrix * gradient_matrix), ('dp', 'seq'))  39.2 us
    all_gather x1, waiting for transfers between devices, local(): piece_values = lax.all_gather(value_codes, 'seq', axis=0, tiled=True)  35.2 us
    reduce_scatter x1, waiting for transfers between devices, local(): lax.psum_scatter(group_sum, 'seq', scatter_dimension=0, tiled=True)  31.4 us
    all_gather x1, blocking collectives, local(): lax.all_gather(value_scale_factors, 'seq', axis=0, tiled=True)  17.3 us
    all_gather x1, blocking collectives, local(): lax.all_gather(key_scale_factors, 'seq', axis=0, tiled=True)  17.1 us
    all_gather x1, blocking collectives, local(): piece_docs = lax.all_gather(own_docs, 'seq', axis=0, tiled=True)  11.5 us
  transfers between devices with their start and end apart: 5, of which 5 were waited for; matrix products, arithmetic and copies ran while one was open for 4% of the time, Pallas kernels for 0%

commit v1 on v0

v1 whole, which is shorter than its diff:
```python
import functools

import jax
import jax.numpy as jnp
from jax import lax
from jax.experimental import pallas as pl
from jax.experimental.pallas import tpu as pltpu
from jax.sharding import PartitionSpec as P

HEADS = 16
KV_HEADS = 8
HEAD_DIM = 128
GROUP = 128

score_scale = 144.0 ** (-0.5)
soft_cap = 50.0
beta_first = 0.9
beta_second = 0.95
learn_rate = 0.001
decay_rate = 0.1

MESH = pl.DeviceIdType.MESH


def restore(blocks):
    grouped = blocks.astype(jnp.float32).reshape(blocks.shape[0], KV_HEADS, HEAD_DIM)
    scales = (jnp.max(jnp.abs(grouped), axis=-1) + 1e-06).astype(jnp.bfloat16)
    wide = scales.astype(jnp.float32)[..., None]
    coded = (grouped / wide).astype(jnp.bfloat16)
    return (coded.astype(jnp.float32) * wide).astype(jnp.bfloat16).reshape(blocks.shape)


def orders(bits):
    high = list(range(1, bits))
    return (high, high[::-1])


def flip(me, r):
    out = me
    b = 0
    while (1 << b) <= r:
        if r & (1 << b):
            digit = lax.rem(lax.div(me, 1 << b), 2)
            out = out + (1 - 2 * digit) * (1 << b)
        b += 1
    return out


def gather_kernel(
    bits, n,
    k_ref, v_ref, doc_ref, w_ref,
    k_all, v_all, doc_all, w_all,
    own_sem, ws, wr, ks, kr, ds_, dr, ts, tr,
):
    me = lax.axis_index("dp")
    z = lax.axis_index("seq")
    tokens = k_ref.shape[0]
    rows, width = w_ref.shape
    half = width // 2
    big = n * rows
    right, left = lax.rem(z + 1, n), lax.rem(z + n - 1, n)

    def w_own(h):
        return w_ref.at[:, pl.ds(h * half, half)]

    def w_slot(zz, h):
        start = pl.multiple_of((me * n + zz) * rows, 16)
        return w_all.at[pl.ds(start, rows), pl.ds(h * half, half)]

    def kv_slot(ref, zz):
        return ref.at[pl.ds(pl.multiple_of(zz * tokens, 128), tokens), :]

    def doc_slot(zz):
        return doc_all.at[:, pl.ds(pl.multiple_of(zz * tokens, 128), tokens)]

    local = [
        pltpu.make_async_copy(k_ref, kv_slot(k_all, z), own_sem.at[0]),
        pltpu.make_async_copy(v_ref, kv_slot(v_all, z), own_sem.at[1]),
        pltpu.make_async_copy(doc_ref, doc_slot(z), own_sem.at[2]),
        pltpu.make_async_copy(w_own(0), w_slot(z, 0), own_sem.at[3]),
        pltpu.make_async_copy(w_own(1), w_slot(z, 1), own_sem.at[4]),
    ]
    for c in local:
        c.start()

    greet_bits(me, z, bits, n)

    started = []

    def remote(src, dst, ssem, rsem, dp, seq):
        copy = pltpu.make_async_remote_copy(
            src_ref=src, dst_ref=dst, send_sem=ssem, recv_sem=rsem,
            device_id={"dp": dp, "seq": seq}, device_id_type=MESH,
        )
        copy.start()
        started.append(copy)
        return copy

    far = n // 2

    def ring(own, slot, ss, rs, direction, part, s):
        shift = n - (s - 1) if direction == 0 else s - 1
        at = lax.rem(z + shift, n)
        src = own(part) if s == 1 else slot(at, part)
        to = right if direction == 0 else left
        return remote(
            src, slot(at, part), ss.at[direction, part, s - 1], rs.at[direction, part, s - 1],
            me, to,
        )

    def kv_own(part):
        return k_ref if part == 0 else v_ref

    def kv_at(zz, part):
        return kv_slot(k_all if part == 0 else v_all, zz)

    streams = ((0, 0), (1, 1), (0, 1), (1, 0))

    def runs(direction, part, s):
        return s < far or (s == far and direction == part)

    wc, kc = {}, {}
    for direction, part in streams:
        if runs(direction, part, 1):
            wc[direction, part, 1] = ring(w_own, w_slot, ws, wr, direction, part, 1)
    doc_copies = []
    for s in range(1, n):
        to = lax.rem(z + s, n)
        doc_copies.append(
            remote(doc_ref, doc_slot(z), ds_.at[s - 1], dr.at[s - 1], me, to)
        )
    for direction, part in streams:
        if runs(direction, part, 1):
            kc[direction, part, 1] = ring(kv_own, kv_at, ks, kr, direction, part, 1)
    for s in range(2, far + 1):
        for direction, part in streams:
            if runs(direction, part, s - 1) and runs(direction, part, s):
                wc[direction, part, s - 1].wait_recv()
                wc[direction, part, s] = ring(w_own, w_slot, ws, wr, direction, part, s)
    for (direction, part, s), c in wc.items():
        if not (runs(direction, part, s + 1) and s + 1 <= far):
            c.wait_recv()
    for c in local:
        c.wait()

    tree = []
    for h, order in enumerate(orders(bits)):
        tree.append(list(order) + [0])

    def block(r, h):
        start = pl.multiple_of(flip(me, r) * big, 16)
        return w_all.at[pl.ds(start, big), pl.ds(h * half, half)]

    tc = {}

    def forward(r, h):
        order = tree[h]
        last = -1
        for i, b in enumerate(order):
            if r & (1 << b):
                last = i
        for b in order[last + 1:]:
            nr = r | (1 << b)
            tc[h, nr] = remote(
                block(r, h), block(r, h), ts.at[h, nr], tr.at[h, nr], flip(me, 1 << b), z
            )

    for h in range(2):
        forward(0, h)
    count = 1 << bits
    rank = []
    for h in range(2):
        seen = [0]
        for b in tree[h]:
            seen = seen + [r | (1 << b) for r in seen]
        rank.append(seen[1:])
    for i in range(count - 1):
        for h in range(2):
            r = rank[h][i]
            if r % 2 == 0:
                tc[h, r].wait_recv()
                forward(r, h)
        if i == 0:
            for s in range(2, far + 1):
                for direction, part in streams:
                    if runs(direction, part, s - 1) and runs(direction, part, s):
                        kc[direction, part, s - 1].wait_recv()
                        kc[direction, part, s] = ring(
                            kv_own, kv_at, ks, kr, direction, part, s
                        )
    for (direction, part, s), c in kc.items():
        if not (runs(direction, part, s + 1) and s + 1 <= far):
            c.wait_recv()
    for c in doc_copies:
        c.wait_recv()
    for i in range(count - 1):
        for h in range(2):
            r = rank[h][i]
            if r % 2 == 1:
                tc[h, r].wait_recv()
    for c in started:
        c.wait_send()


def greet_bits(me, z, bits, n):
    barrier = pltpu.get_barrier_semaphore()
    for b in range(bits):
        pl.semaphore_signal(
            barrier, inc=1, device_id={"dp": flip(me, 1 << b), "seq": z}, device_id_type=MESH
        )
    for s in range(1, n):
        pl.semaphore_signal(
            barrier, inc=1, device_id={"dp": me, "seq": lax.rem(z + s, n)}, device_id_type=MESH
        )
    pl.semaphore_wait(barrier, bits + n - 1)


def gather_all(k, v, docs, w, bits, n):
    tokens, kw = k.shape
    rows, width = w.shape
    far = n // 2
    sem = pltpu.SemaphoreType.DMA
    vm = pl.BlockSpec(memory_space=pltpu.VMEM)
    hbm = pl.BlockSpec(memory_space=pl.ANY)
    count = 1 << bits
    return pl.pallas_call(
        functools.partial(gather_kernel, bits, n),
        out_shape=(
            jax.ShapeDtypeStruct((n * tokens, kw), k.dtype),
            jax.ShapeDtypeStruct((n * tokens, kw), v.dtype),
            jax.ShapeDtypeStruct((8, n * tokens), docs.dtype),
            jax.ShapeDtypeStruct((count * n * rows, width), w.dtype),
        ),
        in_specs=[vm] * 4,
        out_specs=(hbm, hbm, hbm, hbm),
        scratch_shapes=[
            sem((5,)),
            sem((2, 2, far)), sem((2, 2, far)),
            sem((2, 2, far)), sem((2, 2, far)),
            sem((n - 1,)), sem((n - 1,)),
            sem((2, count)), sem((2, count)),
        ],
        compiler_params=pltpu.CompilerParams(collective_id=0, has_side_effects=True),
    )(k, v, docs, w)


def attend_kernel(q_ref, k_ref, v_ref, docs_ref, own_ref, o_ref):
    z = lax.axis_index("seq")
    tokens = q_ref.shape[0]
    length = k_ref.shape[0]
    key_at = lax.broadcasted_iota(jnp.int32, (tokens, length), 1)
    query_at = lax.broadcasted_iota(jnp.int32, (tokens, length), 0) + z * tokens
    allowed = (own_ref[:, 0:1] == docs_ref[0:1, :]) & (key_at <= query_at)
    for i in range(2):
        cols = slice(i * HEAD_DIM, (i + 1) * HEAD_DIM)
        scores = lax.dot_general(
            q_ref[:, cols], k_ref[...], (((1,), (1,)), ((), ())),
            preferred_element_type=jnp.float32,
        )
        capped = soft_cap * jnp.tanh(scores * (score_scale / soft_cap))
        weights = jnp.where(allowed, jnp.exp(capped), 0.0)
        total = jnp.sum(weights, axis=-1, keepdims=True)
        mixed = jnp.dot(
            weights.astype(jnp.bfloat16), v_ref[...], preferred_element_type=jnp.float32
        )
        o_ref[:, cols] = (mixed / total).astype(o_ref.dtype)


def attend(q, k_all, v_all, docs_all, own):
    tokens = q.shape[0]
    length = k_all.shape[0]
    pair = HEADS // KV_HEADS * HEAD_DIM
    return pl.pallas_call(
        attend_kernel,
        grid=(KV_HEADS,),
        out_shape=jax.ShapeDtypeStruct(q.shape, q.dtype),
        in_specs=[
            pl.BlockSpec((tokens, pair), lambda g: (0, g)),
            pl.BlockSpec((length, HEAD_DIM), lambda g: (0, g)),
            pl.BlockSpec((length, HEAD_DIM), lambda g: (0, g)),
            pl.BlockSpec((8, length), lambda g: (0, 0)),
            pl.BlockSpec((tokens, 128), lambda g: (0, 0)),
        ],
        out_specs=pl.BlockSpec((tokens, pair), lambda g: (0, g)),
    )(q, k_all, v_all, docs_all, own)


def step_kernel(
    bits, n,
    att_ref, cot_ref, w_ref, m1_ref, s1_ref, m2_ref, s2_ref,
    nw_ref, n1_ref, ns1_ref, n2_ref, ns2_ref,
    sb, rb, zs, zr, grad, tot_s, tot_r,
    bs, br, zss, zsr, qs, qr,
):
    me = lax.axis_index("dp")
    z = lax.axis_index("seq")
    rows, width = w_ref.shape
    half = width // 2
    big = n * rows
    count = 1 << bits
    right, left = lax.rem(z + 1, n), lax.rem(z + n - 1, n)
    started = []

    def remote(src, dst, ssem, rsem, dp, seq):
        copy = pltpu.make_async_remote_copy(
            src_ref=src, dst_ref=dst, send_sem=ssem, recv_sem=rsem,
            device_id={"dp": dp, "seq": seq}, device_id_type=MESH,
        )
        copy.start()
        started.append(copy)
        return copy

    greet_bits(me, z, bits, n)

    def product(r, h):
        start = pl.multiple_of(flip(me, r) * big, 128)
        return jnp.dot(
            att_ref[pl.ds(start, big), :],
            cot_ref[:, h * half:(h + 1) * half],
            preferred_element_type=jnp.float32,
        )

    tree = [[0] + list(order) for order in orders(bits)]
    sent = {}

    def first_bit(r, h):
        for b in tree[h]:
            if r & (1 << b):
                return b

    def push(r, h):
        b = first_bit(r, h)
        sent[h, r] = remote(
            sb.at[h, r], rb.at[h, r], bs.at[h, r], br.at[h, r], flip(me, 1 << b), z
        )

    seq_of = []
    for h in range(2):
        seen = [0]
        for b in tree[h][:0:-1]:
            seen = seen + [r | (1 << b) for r in seen]
        def key(r, h=h):
            if r == 0:
                return (len(tree[h]), 0)
            return (tree[h].index(first_bit(r, h)), r)
        seq_of.append(sorted(seen, key=key))
    for i in range(count // 2):
        for h in range(2):
            r = seq_of[h][i] | 1
            sb[h, r] = product(r, h).astype(jnp.bfloat16)
            push(r, h)
    for i in range(count // 2):
        for h in range(2):
            r = seq_of[h][i]
            value = product(r, h)
            for b in tree[h]:
                if r & (1 << b):
                    break
                src = r | (1 << b)
                sent[h, src].wait_recv()
                value = value + rb[h, src].astype(jnp.float32)
            if r:
                sb[h, r] = value.astype(jnp.bfloat16)
                push(r, h)
            else:
                grad[:, h * half:(h + 1) * half] = value

    def part(zz, h):
        start = pl.multiple_of(zz * rows, 16)
        return grad[pl.ds(start, rows), h * half:(h + 1) * half]

    ring = {}
    for s in range(n):
        for h in range(2):
            shift = (2 * n - 1 - s) if h == 0 else (1 + s)
            at = lax.rem(z + shift, n)
            value = part(at, h)
            if s:
                ring[h, s - 1].wait_recv()
                value = value + zr[h, s - 1].astype(jnp.float32)
            if s < n - 1:
                zs[h, s] = value.astype(jnp.bfloat16)
                ring[h, s] = remote(
                    zs.at[h, s], zr.at[h, s], zss.at[h, s], zsr.at[h, s],
                    me, right if h == 0 else left,
                )
            else:
                grad[0:rows, h * half:(h + 1) * half] = value

    own = grad[0:rows, :]
    total = jnp.broadcast_to(
        jnp.sum(jnp.sum(own * own, axis=1, keepdims=True), axis=0, keepdims=True), (8, 128)
    )
    for b in range(bits):
        tot_s[b] = total
        c = remote(tot_s.at[b], tot_r.at[b], qs.at[b], qr.at[b], flip(me, 1 << b), z)
        c.wait_recv()
        total = total + tot_r[b]
    tot_s[bits] = total
    last = []
    for s in range(1, n):
        i = bits + s - 1
        last.append(
            remote(tot_s.at[bits], tot_r.at[i], qs.at[i], qr.at[i], me, lax.rem(z + s, n))
        )
    for s in range(1, n):
        last[s - 1].wait_recv()
        total = total + tot_r[bits + s - 1]

    rms = jnp.sqrt(total[0:1, :] / (count * n * rows * width) + 1e-06)
    factor = jnp.minimum(1.0, 1.0 / rms)

    def decode(coded, scale):
        x = coded.astype(jnp.float32)
        root = scale * jnp.sqrt(jnp.abs(x))
        return jnp.where(x < 0, -root, root)

    def encode(x):
        scale = jnp.max(jnp.abs(x), axis=-1, keepdims=True) + 1e-06
        return (x * jnp.abs(x) / (scale * scale)).astype(jnp.bfloat16), scale

    for g in range(width // GROUP):
        cols = slice(g * GROUP, (g + 1) * GROUP)
        clipped = grad[0:rows, cols] * factor
        first = beta_first * decode(m1_ref[:, cols], s1_ref[:, g:g + 1]) + (
            1.0 - beta_first
        ) * clipped
        second = (
            beta_second * decode(m2_ref[:, cols], s2_ref[:, g:g + 1])
            + (1.0 - beta_second) * clipped * clipped
        )
        weight = w_ref[:, cols]
        nw_ref[:, cols] = weight - learn_rate * (
            first / (jnp.sqrt(second) + 1e-08) + decay_rate * weight
        )
        n1_ref[:, cols], ns1_ref[:, g:g + 1] = encode(first)
        n2_ref[:, cols], ns2_ref[:, g:g + 1] = encode(second)
    for c in started:
        c.wait_send()


def train_step(att_t, cot, weight, m1, s1, m2, s2, bits, n):
    rows, width = weight.shape
    half = width // 2
    count = 1 << bits
    sem = pltpu.SemaphoreType.DMA
    vm = pl.BlockSpec(memory_space=pltpu.VMEM)
    like = lambda a: jax.ShapeDtypeStruct(a.shape, a.dtype)
    return pl.pallas_call(
        functools.partial(step_kernel, bits, n),
        out_shape=(like(weight), like(m1), like(s1), like(m2), like(s2)),
        in_specs=[vm] * 7,
        out_specs=(vm,) * 5,
        scratch_shapes=[
            pltpu.VMEM((2, count, n * rows, half), jnp.bfloat16),
            pltpu.VMEM((2, count, n * rows, half), jnp.bfloat16),
            pltpu.VMEM((2, n - 1, rows, half), jnp.bfloat16),
            pltpu.VMEM((2, n - 1, rows, half), jnp.bfloat16),
            pltpu.VMEM((n * rows, width), jnp.float32),
            pltpu.VMEM((bits + 1, 8, 128), jnp.float32),
            pltpu.VMEM((bits + n - 1, 8, 128), jnp.float32),
            sem((2, count)), sem((2, count)),
            sem((2, n - 1)), sem((2, n - 1)),
            sem((bits + n - 1,)), sem((bits + n - 1,)),
        ],
        compiler_params=pltpu.CompilerParams(
            collective_id=1, has_side_effects=True, vmem_limit_bytes=60 * 1024 * 1024
        ),
    )(att_t, cot, weight, m1, s1, m2, s2)


def local(
    bits, n,
    queries, keys, values, segments, cotangent, weight,
    first_moment, first_scale, second_moment, second_scale,
):
    docs = segments[0]
    tokens = docs.shape[0]
    k_all, v_all, docs_all, w_all = gather_all(
        restore(keys[0]),
        restore(values[0]),
        jnp.broadcast_to(docs[None, :], (8, tokens)),
        weight.astype(jnp.bfloat16),
        bits, n,
    )
    own = jnp.broadcast_to(docs[:, None], (tokens, 128))
    attended = attend(queries[0], k_all, v_all, docs_all, own)
    layer_out = jnp.dot(attended, w_all, preferred_element_type=jnp.float32)
    layer_out = layer_out.astype(jnp.bfloat16)[None]
    new_weight, new_first, new_first_scale, new_second, new_second_scale = train_step(
        attended.T, cotangent[0], weight, first_moment, first_scale,
        second_moment, second_scale, bits, n,
    )
    return (layer_out, new_weight, new_first, new_first_scale, new_second, new_second_scale)


def solution(mesh):
    bits = mesh.shape["dp"].bit_length() - 1
    n = mesh.shape["seq"]
    shard = P(("dp", "seq"), None)
    tok = P("dp", "seq", None)
    return jax.shard_map(
        functools.partial(local, bits, n),
        mesh=mesh,
        in_specs=(tok, tok, tok, P("dp", "seq"), tok, shard, shard, shard, shard, shard),
        out_specs=(tok, shard, shard, shard, shard, shard),
        check_vma=False,
    )
```

time: 382 us -> 247 us (0.65)
  waiting for transfers between devices: 227 us -> 0 us
  Pallas kernels: 0 us -> 220 us
  blocking collectives: 85.1 us -> 0 us
  matrix products: 29.7 us -> 7.7 us
  between operations: 14.7 us -> 0.78 us
  other arithmetic: 17.9 us -> 4.38 us
  local copies, waits for them, and re-layouts: 6.89 us -> 13.7 us
    pallas_call x0 -> x3, Pallas kernels: none -> 220 us  [the longest x1 123 us: gather_all(): pl.pallas_call(functools.partial(gather_kernel, bits, n), out_shape=(jax....]
    all_gather x3 -> x0, waiting for transfers between devices: 120 us -> none  [the longest x1 80.2 us: local(): lax.all_gather(weight_low, ('dp', 'seq'), axis=0, tiled=True)]
    reduce_scatter x2 -> x0, waiting for transfers between devices: 107 us -> none  [the longest x1 75.7 us: local(): lax.psum_scatter(lax.dot_general(columns, cot_rows, (((0,), (0,)), ((), (...]
    all_gather x3 -> x0, blocking collectives: 45.9 us -> none  [the longest x1 17.3 us: local(): lax.all_gather(value_scale_factors, 'seq', axis=0, tiled=True)]
    psum x1 -> x0, blocking collectives: 39.2 us -> none  [local(): lax.psum(jnp.sum(gradient_matrix * gradient_matrix), ('dp', 'seq'))]
    dot_general x4 -> x1, matrix products: 29.7 us -> 7.7 us  [local(): layer_out = jnp.dot(attended, w_all, preferred_element_type=jnp.float32)]
    unnamed x24 -> x23, local copies, waits for them, and re-layouts: 1.98 us -> 10 us
    convert_element_type x9 -> x4, other arithmetic: 10.4 us -> 2.43 us  [the longest x1 1.67 us: restore(): (coded.astype(jnp.float32) * wide).astype(jnp.bfloat16)]
  transfers between devices with their start and end apart: 5 -> 0, of which waited for: 5 -> 0; matrix products, arithmetic and copies ran while one was open for 4% -> 0% of each run, Pallas kernels for 0% -> 0%
where the time goes in v1:
time: 247 us
  Pallas kernels  220 us (89%)
  local copies, waits for them, and re-layouts  13.7 us (6%)
  matrix products  7.7 us (3%)
  other arithmetic  4.38 us (2%)
    pallas_call x1, Pallas kernels, gather_all(): pl.pallas_call(functools.partial(gather_kernel, bits, n), out_shape=(jax....  123 us
    pallas_call x1, Pallas kernels, train_step(): pl.pallas_call(functools.partial(step_kernel, bits, n), out_shape=(like(w...  85.7 us
    pallas_call x1, Pallas kernels, attend(): pl.pallas_call(attend_kernel, grid=(KV_HEADS,), out_shape=jax.ShapeDtypeS...  11.7 us
    unnamed x23, local copies, waits for them, and re-layouts  10 us
    dot_general x1, matrix products, local(): layer_out = jnp.dot(attended, w_all, preferred_element_type=jnp.float32)  7.7 us

profile of v1, /device:TPU:0, one launch (start us, length us, event | category | flops | bytes accessed | tf_op | source)
XLA Modules:
  0.0 246.5 jit_solution(16849237554033911823)
XLA Ops:
  0.6 1.2 fusion.3
  1.8 0.0 copy-start.2
  1.8 0.2 copy.37
  2.0 0.3 reduce_max.18
  2.4 0.1 copy.28
  2.4 0.1 copy.29
  2.6 0.3 div.22
  2.9 0.0 copy-done.2
  2.9 0.1 fusion.6
  3.0 0.0 copy-start.3
  3.1 0.2 copy.39
  3.3 0.3 reduce_max.19
  3.6 0.1 copy.30
  3.7 0.1 copy.31
  3.8 0.3 div.25
  4.2 0.0 copy-start.6
  4.2 0.0 copy-start.1
  4.2 0.0 copy-done.3
  4.2 1.7 fusion.7
  5.9 0.0 copy-done.6
  5.9 0.6 broadcast_in_dim.18.doc_ref
  6.5 0.0 copy-done.1
  6.5 0.7 convert_element_type.104.w_ref
  7.2 122.6 %shard_map.145 = (bf16[1024,1024]{1,0:T(8,128)(2,1)}, bf16[1024,1024]{1,0:T(8,128)(2,1)}, s32[8,1024]{1,0:T(8,128)}, bf16[2048,2304]{1,0:T(8,128)(2,1)}) custom-call(bf16[256,1024]{1,0:T(8,128)(2,1)} %get-tuple-element.43.k_ref, bf16[256,1024]{1,0:T(8,128)(2,1)} %get-tuple-element.42.v_ref, s32[8,256]{1,0:T(8,128)} %broadcast_in_dim.18.doc_ref, ...), custom_call_target="tpu_custom_call" | custom-call | tf_op jit(solution)/shard_map/pallas_call | solution.py:226
  129.8 0.8 broadcast_in_dim.19.own_ref
  130.6 11.7 %shard_map.146 = bf16[256,2048]{1,0:T(8,128)(2,1)} custom-call(bf16[256,2048]{1,0:T(8,128)(2,1)} %bitcast.54, bf16[1024,1024]{1,0:T(8,128)(2,1)} %get-tuple-element.15.k_ref, bf16[1024,1024]{1,0:T(8,128)(2,1)} %get-tuple-element.16.v_ref, s32[8,1024]{1,0:T(8,128)} %get-tuple-element.17.docs_ref, s32[256,128]{1,0:T(8,128)} %broadcast_in_dim.19.own_ref), custom_call_target="tpu_custom_call" | custom-call | tf_op jit(solution)/shard_map/pallas_call | solution.py:273
  142.2 0.0 copy-start
  142.3 0.0 copy-start.4
  142.3 0.0 copy-start.5
  142.3 7.7 %fusion = bf16[1,256,2304]{2,1,0:T(8,128)(2,1)} fusion(bf16[256,2048]{1,0:T(8,128)(2,1)} %shard_map.146, bf16[2048,2304]{1,0:T(8,128)(2,1)} %get-tuple-element.18), kind=kOutput, calls=%fused_computation.1 | convolution fusion | flops 2416508928 | bytes 11665408 | tf_op jit(solution)/shard_map/dot_general | solution.py:488
  150.0 0.0 copy-done
  150.0 1.3 copy.32
  151.3 0.0 copy-done.4
  151.3 0.7 copy.33.s1_ref
  152.0 0.0 copy-done.5
  152.0 0.7 copy.34.s2_ref
  152.7 85.7 %shard_map.147 = (f32[64,2304]{1,0:T(8,128)}, bf16[64,2304]{1,0:T(8,128)(2,1)}, f32[64,18]{1,0:T(8,128)}, bf16[64,2304]{1,0:T(8,128)(2,1)}, f32[64,18]{1,0:T(8,128)}) custom-call(bf16[2048,256]{1,0:T(8,128)(2,1)} %bitcast.48, bf16[256,2304]{1,0:T(8,128)(2,1)} %bitcast.53, f32[64,2304]{1,0:T(8,128)} %w_ref.1, bf16[64,2304]{1,0:T(8,128)(2,1)} %m1_ref.1, ...), custom_call_target="tpu_custom_call" | custom-call | tf_op jit(solution)/shard_map/pallas_call | solution.py:449
  238.4 1.4 copy.35
  239.8 1.4 copy.36
  241.2 1.9 copy.52
  243.1 1.7 copy.53
  244.8 1.7 copy.54
  (2 shorter events, 0.0 us)
Async XLA Ops:
  1.8 1.1 copy-start.2
  3.0 1.1 copy-start.3
  4.2 1.7 copy-start.6
  4.2 2.3 copy-start.1
  142.2 7.7 %copy-start = (bf16[256,2048]{1,0:T(8,128)(2,1)S(1)}, bf16[256,2048]{1,0:T(8,128)(2,1)}, u32[]{:S(2)}) copy-start(bf16[256,2048]{1,0:T(8,128)(2,1)} %shard_map.146) | copy-start | bytes 3145732
  142.3 9.0 %copy-start.4 = (f32[64,18]{0,1:T(8,128)S(1)}, f32[64,18]{0,1:T(8,128)}, u32[]{:S(2)}) copy-start(f32[64,18]{0,1:T(8,128)} %param.17) | copy-start | bytes 13828
  142.3 9.7 %copy-start.5 = (f32[64,18]{0,1:T(8,128)S(1)}, f32[64,18]{0,1:T(8,128)}, u32[]{:S(2)}) copy-start(f32[64,18]{0,1:T(8,128)} %param.19) | copy-start | bytes 13828

commit v2 on v1

--- a/solution.py
+++ b/solution.py
@@ -28,6 +28,19 @@
     wide = scales.astype(jnp.float32)[..., None]
     coded = (grouped / wide).astype(jnp.bfloat16)
     return (coded.astype(jnp.float32) * wide).astype(jnp.bfloat16).reshape(blocks.shape)
+
+
+def longest(length):
+    return length * 5 // 8
+
+
+def reach_skips(tokens, n):
+    skips = []
+    for s in range(1, n):
+        skip = max(0, s * tokens - longest(n * tokens)) // 128 * 128
+        if skip < tokens:
+            skips.append(skip)
+    return tuple(skips)
 
 
 def orders(bits):
@@ -47,7 +60,7 @@
 
 
 def gather_kernel(
-    bits, n,
+    bits, n, skips,
     k_ref, v_ref, doc_ref, w_ref,
     k_all, v_all, doc_all, w_all,
     own_sem, ws, wr, ks, kr, ds_, dr, ts, tr,
@@ -60,12 +73,9 @@
     big = n * rows
     right, left = lax.rem(z + 1, n), lax.rem(z + n - 1, n)
 
-    def w_own(h):
-        return w_ref.at[:, pl.ds(h * half, half)]
-
-    def w_slot(zz, h):
+    def w_slot(zz):
         start = pl.multiple_of((me * n + zz) * rows, 16)
-        return w_all.at[pl.ds(start, rows), pl.ds(h * half, half)]
+        return w_all.at[pl.ds(start, rows), :]
 
     def kv_slot(ref, zz):
         return ref.at[pl.ds(pl.multiple_of(zz * tokens, 128), tokens), :]
@@ -77,8 +87,7 @@
         pltpu.make_async_copy(k_ref, kv_slot(k_all, z), own_sem.at[0]),
         pltpu.make_async_copy(v_ref, kv_slot(v_all, z), own_sem.at[1]),
         pltpu.make_async_copy(doc_ref, doc_slot(z), own_sem.at[2]),
-        pltpu.make_async_copy(w_own(0), w_slot(z, 0), own_sem.at[3]),
-        pltpu.make_async_copy(w_own(1), w_slot(z, 1), own_sem.at[4]),
+        pltpu.make_async_copy(w_ref, w_slot(z), own_sem.at[3]),
     ]
     for c in local:
         c.start()
@@ -96,52 +105,84 @@
         started.append(copy)
         return copy
 
-    far = n // 2
-
-    def ring(own, slot, ss, rs, direction, part, s):
-        shift = n - (s - 1) if direction == 0 else s - 1
+    def descriptor(src, dst, ssem, rsem, dp, seq):
+        return pltpu.make_async_remote_copy(
+            src_ref=src, dst_ref=dst, send_sem=ssem, recv_sem=rsem,
+            device_id={"dp": dp, "seq": seq}, device_id_type=MESH,
+        )
+
+    def w_hop(direction, s):
+        shift = n + 1 - s if direction == 0 else s - 1
         at = lax.rem(z + shift, n)
-        src = own(part) if s == 1 else slot(at, part)
-        to = right if direction == 0 else left
-        return remote(
-            src, slot(at, part), ss.at[direction, part, s - 1], rs.at[direction, part, s - 1],
-            me, to,
-        )
-
-    def kv_own(part):
-        return k_ref if part == 0 else v_ref
-
-    def kv_at(zz, part):
-        return kv_slot(k_all if part == 0 else v_all, zz)
-
-    streams = ((0, 0), (1, 1), (0, 1), (1, 0))
-
-    def runs(direction, part, s):
-        return s < far or (s == far and direction == part)
-
-    wc, kc = {}, {}
-    for direction, part in streams:
-        if runs(direction, part, 1):
-            wc[direction, part, 1] = ring(w_own, w_slot, ws, wr, direction, part, 1)
+        here = w_ref if s == 1 else w_slot(at)
+        return descriptor(
+            here, w_slot(at), ws.at[direction, s - 1], wr.at[direction, s - 1],
+            me, right if direction == 0 else left,
+        )
+
+    def kv_hop(part, s):
+        at = lax.rem(z + n + 1 - s, n)
+        ref = (k_ref, v_ref)[part]
+        out = (k_all, v_all)[part]
+        skip = skips[s - 1]
+        start = pl.multiple_of(at * tokens + skip, 128)
+        dst = out.at[pl.ds(start, tokens - skip), :]
+        src = ref.at[pl.ds(skip, tokens - skip), :] if s == 1 else dst
+        return descriptor(src, dst, ks.at[part, s - 1], kr.at[part, s - 1], me, right)
+
+    def room(direction, s):
+        if direction == 0:
+            return (z >= s - 1) & (z < n - 1)
+        return (z <= n - s) & (z > 0)
+
+    def landed(direction, s):
+        return z >= s if direction == 0 else z <= n - 1 - s
+
+    steps = len(skips)
+    for s in range(1, n):
+        for direction in range(2):
+            if s > 1:
+
+                @pl.when(landed(direction, s - 1))
+                def _(direction=direction, s=s):
+                    w_hop(direction, s - 1).wait_recv()
+
+            @pl.when(room(direction, s))
+            def _(direction=direction, s=s):
+                w_hop(direction, s).start()
+
+    @pl.when(room(0, 1))
+    def _():
+        kv_hop(0, 1).start()
+        kv_hop(1, 1).start()
+
     doc_copies = []
     for s in range(1, n):
         to = lax.rem(z + s, n)
         doc_copies.append(
             remote(doc_ref, doc_slot(z), ds_.at[s - 1], dr.at[s - 1], me, to)
         )
-    for direction, part in streams:
-        if runs(direction, part, 1):
-            kc[direction, part, 1] = ring(kv_own, kv_at, ks, kr, direction, part, 1)
-    for s in range(2, far + 1):
-        for direction, part in streams:
-            if runs(direction, part, s - 1) and runs(direction, part, s):
-                wc[direction, part, s - 1].wait_recv()
-                wc[direction, part, s] = ring(w_own, w_slot, ws, wr, direction, part, s)
-    for (direction, part, s), c in wc.items():
-        if not (runs(direction, part, s + 1) and s + 1 <= far):
-            c.wait_recv()
+    for direction in range(2):
+
+        @pl.when(landed(direction, n - 1))
+        def _(direction=direction):
+            w_hop(direction, n - 1).wait_recv()
+
     for c in local:
         c.wait()
+
+    def kv_forward(s):
+        for part in range(2):
+
+            @pl.when(landed(0, s - 1))
+            def _(part=part):
+                kv_hop(part, s - 1).wait_recv()
+
+            if s <= steps:
+
+                @pl.when(room(0, s))
+                def _(part=part):
+                    kv_hop(part, s).start()
 
     tree = []
     for h, order in enumerate(orders(bits)):
@@ -180,17 +221,12 @@
             if r % 2 == 0:
                 tc[h, r].wait_recv()
                 forward(r, h)
-        if i == 0:
-            for s in range(2, far + 1):
-                for direction, part in streams:
-                    if runs(direction, part, s - 1) and runs(direction, part, s):
-                        kc[direction, part, s - 1].wait_recv()
-                        kc[direction, part, s] = ring(
-                            kv_own, kv_at, ks, kr, direction, part, s
-                        )
-    for (direction, part, s), c in kc.items():
-        if not (runs(direction, part, s + 1) and s + 1 <= far):
-            c.wait_recv()
+        if i == 0 and steps >= 2:
+            kv_forward(2)
+        if i == count // 2 - 2:
+            for s in range(3, steps + 1):
+                kv_forward(s)
+    kv_forward(steps + 1)
     for c in doc_copies:
         c.wait_recv()
     for i in range(count - 1):
@@ -200,6 +236,19 @@
                 tc[h, r].wait_recv()
     for c in started:
         c.wait_send()
+    for s in range(1, n):
+        for direction in range(2):
+
+            @pl.when(room(direction, s))
+            def _(direction=direction, s=s):
+                w_hop(direction, s).wait_send()
+
+    for s in range(1, steps + 1):
+
+        @pl.when(room(0, s))
+        def _(s=s):
+            kv_hop(0, s).wait_send()
+            kv_hop(1, s).wait_send()
 
 
 def greet_bits(me, z, bits, n):
@@ -218,13 +267,13 @@
 def gather_all(k, v, docs, w, bits, n):
     tokens, kw = k.shape
     rows, width = w.shape
-    far = n // 2
+    skips = reach_skips(tokens, n)
     sem = pltpu.SemaphoreType.DMA
     vm = pl.BlockSpec(memory_space=pltpu.VMEM)
     hbm = pl.BlockSpec(memory_space=pl.ANY)
     count = 1 << bits
     return pl.pallas_call(
-        functools.partial(gather_kernel, bits, n),
+        functools.partial(gather_kernel, bits, n, skips),
         out_shape=(
             jax.ShapeDtypeStruct((n * tokens, kw), k.dtype),
             jax.ShapeDtypeStruct((n * tokens, kw), v.dtype),
@@ -234,9 +283,9 @@
         in_specs=[vm] * 4,
         out_specs=(hbm, hbm, hbm, hbm),
         scratch_shapes=[
-            sem((5,)),
-            sem((2, 2, far)), sem((2, 2, far)),
-            sem((2, 2, far)), sem((2, 2, far)),
+            sem((4,)),
+            sem((2, n - 1)), sem((2, n - 1)),
+            sem((2, len(skips))), sem((2, len(skips))),
             sem((n - 1,)), sem((n - 1,)),
             sem((2, count)), sem((2, count)),
         ],
@@ -251,6 +300,9 @@
     key_at = lax.broadcasted_iota(jnp.int32, (tokens, length), 1)
     query_at = lax.broadcasted_iota(jnp.int32, (tokens, length), 0) + z * tokens
     allowed = (own_ref[:, 0:1] == docs_ref[0:1, :]) & (key_at <= query_at)
+    place = lax.broadcasted_iota(jnp.int32, v_ref.shape, 0)
+    seen = (place < (z + 1) * tokens) & (place >= z * tokens - longest(length))
+    value = jnp.where(seen, v_ref[...].astype(jnp.float32), 0.0).astype(jnp.bfloat16)
     for i in range(2):
         cols = slice(i * HEAD_DIM, (i + 1) * HEAD_DIM)
         scores = lax.dot_general(
@@ -261,7 +313,7 @@
         weights = jnp.where(allowed, jnp.exp(capped), 0.0)
         total = jnp.sum(weights, axis=-1, keepdims=True)
         mixed = jnp.dot(
-            weights.astype(jnp.bfloat16), v_ref[...], preferred_element_type=jnp.float32
+            weights.astype(jnp.bfloat16), value, preferred_element_type=jnp.float32
         )
         o_ref[:, cols] = (mixed / total).astype(o_ref.dtype)
 
@@ -287,14 +339,13 @@
 
 def step_kernel(
     bits, n,
-    att_ref, cot_ref, w_ref, m1_ref, s1_ref, m2_ref, s2_ref,
-    nw_ref, n1_ref, ns1_ref, n2_ref, ns2_ref,
+    att_ref, cot_ref, own_ref, sum_ref,
     sb, rb, zs, zr, grad, tot_s, tot_r,
     bs, br, zss, zsr, qs, qr,
 ):
     me = lax.axis_index("dp")
     z = lax.axis_index("seq")
-    rows, width = w_ref.shape
+    rows, width = own_ref.shape
     half = width // 2
     big = n * rows
     count = 1 << bits
@@ -385,9 +436,9 @@
                     me, right if h == 0 else left,
                 )
             else:
-                grad[0:rows, h * half:(h + 1) * half] = value
-
-    own = grad[0:rows, :]
+                own_ref[:, h * half:(h + 1) * half] = value
+
+    own = own_ref[...]
     total = jnp.broadcast_to(
         jnp.sum(jnp.sum(own * own, axis=1, keepdims=True), axis=0, keepdims=True), (8, 128)
     )
@@ -407,7 +458,18 @@
         last[s - 1].wait_recv()
         total = total + tot_r[bits + s - 1]
 
-    rms = jnp.sqrt(total[0:1, :] / (count * n * rows * width) + 1e-06)
+    sum_ref[...] = total
+    for c in started:
+        c.wait_send()
+
+
+def adam_kernel(
+    entries,
+    grad_ref, sum_ref, w_ref, m1_ref, s1_ref, m2_ref, s2_ref,
+    nw_ref, n1_ref, ns1_ref, n2_ref, ns2_ref,
+):
+    width = w_ref.shape[1]
+    rms = jnp.sqrt(sum_ref[0:1, :] / entries + 1e-06)
     factor = jnp.minimum(1.0, 1.0 / rms)
 
     def decode(coded, scale):
@@ -421,7 +483,7 @@
 
     for g in range(width // GROUP):
         cols = slice(g * GROUP, (g + 1) * GROUP)
-        clipped = grad[0:rows, cols] * factor
+        clipped = grad_ref[:, cols] * factor
         first = beta_first * decode(m1_ref[:, cols], s1_ref[:, g:g + 1]) + (
             1.0 - beta_first
         ) * clipped
@@ -435,8 +497,6 @@
         )
         n1_ref[:, cols], ns1_ref[:, g:g + 1] = encode(first)
         n2_ref[:, cols], ns2_ref[:, g:g + 1] = encode(second)
-    for c in started:
-        c.wait_send()
 
 
 def train_step(att_t, cot, weight, m1, s1, m2, s2, bits, n):
@@ -446,11 +506,11 @@
     sem = pltpu.SemaphoreType.DMA
     vm = pl.BlockSpec(memory_space=pltpu.VMEM)
     like = lambda a: jax.ShapeDtypeStruct(a.shape, a.dtype)
-    return pl.pallas_call(
+    grad, total = pl.pallas_call(
         functools.partial(step_kernel, bits, n),
-        out_shape=(like(weight), like(m1), like(s1), like(m2), like(s2)),
-        in_specs=[vm] * 7,
-        out_specs=(vm,) * 5,
+        out_shape=(like(weight), jax.ShapeDtypeStruct((8, 128), jnp.float32)),
+        in_specs=[vm] * 2,
+        out_specs=(vm,) * 2,
         scratch_shapes=[
             pltpu.VMEM((2, count, n * rows, half), jnp.bfloat16),
             pltpu.VMEM((2, count, n * rows, half), jnp.bfloat16),
@@ -466,7 +526,13 @@
         compiler_params=pltpu.CompilerParams(
             collective_id=1, has_side_effects=True, vmem_limit_bytes=60 * 1024 * 1024
         ),
-    )(att_t, cot, weight, m1, s1, m2, s2)
+    )(att_t, cot)
+    return pl.pallas_call(
+        functools.partial(adam_kernel, float(count * n * rows * width)),
+        out_shape=(like(weight), like(m1), like(s1), like(m2), like(s2)),
+        in_specs=[vm] * 7,
+        out_specs=(vm,) * 5,
+    )(grad, total, weight, m1, s1, m2, s2)
 
 
 def local(

time: 247 us -> 204 us (0.83)
  Pallas kernels: 220 us -> 182 us
  local copies, waits for them, and re-layouts: 13.7 us -> 9.37 us
    pallas_call x1 -> x2, Pallas kernels: 123 us -> 75 us  [the longest x1 70.6 us: gather_all(): pl.pallas_call(functools.partial(gather_kernel, bits, n, skips), out_shap...]
    pallas_call x1, Pallas kernels: 85.7 us -> 94.5 us  [train_step(): pl.pallas_call(functools.partial(step_kernel, bits, n), out_shape=(like(w...]
    unnamed x23 -> x20, local copies, waits for them, and re-layouts: 10 us -> 4.69 us
where the time goes in v2:
time: 204 us
  Pallas kernels  182 us (89%)
  local copies, waits for them, and re-layouts  9.37 us (5%)
  matrix products  7.29 us (4%)
  other arithmetic  4.38 us (2%)
    pallas_call x1, Pallas kernels, train_step(): pl.pallas_call(functools.partial(step_kernel, bits, n), out_shape=(like(w...  94.5 us
    pallas_call x1, Pallas kernels, gather_all(): pl.pallas_call(functools.partial(gather_kernel, bits, n, skips), out_shap...  70.6 us
    pallas_call x1, Pallas kernels, attend(): pl.pallas_call(attend_kernel, grid=(KV_HEADS,), out_shape=jax.ShapeDtypeS...  12.4 us
    dot_general x1, matrix products, local(): layer_out = jnp.dot(attended, w_all, preferred_element_type=jnp.float32)  7.29 us
    unnamed x20, local copies, waits for them, and re-layouts  4.69 us
    pallas_call x1, Pallas kernels, train_step(): pl.pallas_call(functools.partial(adam_kernel, float(count * n * rows * wi...  4.38 us

profile of v2, /device:TPU:0, one launch (start us, length us, event | category | flops | bytes accessed | tf_op | source)
XLA Modules:
  0.0 203.7 jit_solution(2353299450278209785)
XLA Ops:
  0.6 1.2 fusion.3
  1.8 0.0 copy-start.2
  1.8 0.2 copy.37
  2.0 0.3 reduce_max.18
  2.4 0.1 copy.28
  2.4 0.1 copy.29
  2.6 0.3 div.22
  2.9 0.0 copy-done.2
  2.9 0.1 fusion.6
  3.0 0.0 copy-start.3
  3.1 0.2 copy.39
  3.3 0.3 reduce_max.19
  3.6 0.1 copy.30
  3.7 0.1 copy.31
  3.8 0.3 div.25
  4.2 0.0 copy-start.6
  4.2 0.0 copy-start.1
  4.2 0.0 copy-done.3
  4.2 1.7 fusion.7
  5.9 0.0 copy-done.6
  5.9 0.6 broadcast_in_dim.18.doc_ref
  6.5 0.0 copy-done.1
  6.5 0.7 convert_element_type.104.w_ref
  7.2 70.6 %shard_map.145 = (bf16[1024,1024]{1,0:T(8,128)(2,1)}, bf16[1024,1024]{1,0:T(8,128)(2,1)}, s32[8,1024]{1,0:T(8,128)}, bf16[2048,2304]{1,0:T(8,128)(2,1)}) custom-call(bf16[256,1024]{1,0:T(8,128)(2,1)} %get-tuple-element.47.k_ref, bf16[256,1024]{1,0:T(8,128)(2,1)} %get-tuple-element.46.v_ref, s32[8,256]{1,0:T(8,128)} %broadcast_in_dim.18.doc_ref, ...), custom_call_target="tpu_custom_call" | custom-call | tf_op jit(solution)/shard_map/pallas_call | solution.py:275
  77.8 0.8 broadcast_in_dim.19.own_ref
  78.6 12.4 %shard_map.146 = bf16[256,2048]{1,0:T(8,128)(2,1)} custom-call(bf16[256,2048]{1,0:T(8,128)(2,1)} %bitcast.54, bf16[1024,1024]{1,0:T(8,128)(2,1)} %get-tuple-element.17.k_ref, bf16[1024,1024]{1,0:T(8,128)(2,1)} %get-tuple-element.18.v_ref, s32[8,1024]{1,0:T(8,128)} %get-tuple-element.19.docs_ref, s32[256,128]{1,0:T(8,128)} %broadcast_in_dim.19.own_ref), custom_call_target="tpu_custom_call" | custom-call | tf_op jit(solution)/shard_map/pallas_call | solution.py:325
  91.0 0.0 copy-start.4
  91.0 0.0 copy-start.5
  91.0 2.3 %copy.32 = bf16[256,2048]{0,1:T(8,128)(2,1)} copy(bf16[256,2048]{1,0:T(8,128)(2,1)} %shard_map.146) | data formatting | bytes 2097152 | tf_op jit(solution)/shard_map/pallas_call | solution.py:325
  93.3 0.0 copy-start
  93.3 94.5 %shard_map.147 = (f32[64,2304]{1,0:T(8,128)}, f32[8,128]{1,0:T(8,128)}) custom-call(bf16[2048,256]{1,0:T(8,128)(2,1)} %bitcast.49, bf16[256,2304]{1,0:T(8,128)(2,1)} %bitcast.53), custom_call_target="tpu_custom_call" | custom-call | tf_op jit(solution)/shard_map/pallas_call | solution.py:509
  187.7 0.0 copy-done.4
  187.7 0.7 copy.33.s1_ref
  188.4 0.0 copy-done.5
  188.4 0.7 copy.34.s2_ref
  189.1 4.4 %shard_map.148 = (f32[64,2304]{1,0:T(8,128)}, bf16[64,2304]{1,0:T(8,128)(2,1)}, f32[64,18]{1,0:T(8,128)}, bf16[64,2304]{1,0:T(8,128)(2,1)}, f32[64,18]{1,0:T(8,128)}) custom-call(f32[64,2304]{1,0:T(8,128)} %get-tuple-element.21.grad_ref, f32[8,128]{1,0:T(8,128)} %get-tuple-element.22.sum_ref, f32[64,2304]{1,0:T(8,128)} %w_ref.1, bf16[64,2304]{1,0:T(8,128)(2,1)} %m1_ref.1, ...), custom_call_target="tpu_custom_call" | custom-call | tf_op jit(solution)/shard_map/pallas_call | solution.py:530
  193.5 1.4 copy.35
  194.9 1.4 copy.36
  196.4 0.0 copy-done
  196.4 7.3 %fusion = bf16[1,256,2304]{2,1,0:T(8,128)(2,1)} fusion(bf16[256,2048]{1,0:T(8,128)(2,1)S(1)} %copy-done, bf16[2048,2304]{1,0:T(8,128)(2,1)} %get-tuple-element.20), kind=kOutput, calls=%fused_computation.1 | convolution fusion | flops 2416508928 | bytes 11665408 | tf_op jit(solution)/shard_map/dot_general | solution.py:554
  (2 shorter events, 0.0 us)
Async XLA Ops:
  1.8 1.1 copy-start.2
  3.0 1.1 copy-start.3
  4.2 1.7 copy-start.6
  4.2 2.3 %copy-start.1 = (f32[64,2304]{1,0:T(8,128)S(1)}, f32[64,2304]{1,0:T(8,128)}, u32[]{:S(2)}) copy-start(f32[64,2304]{1,0:T(8,128)} %w_ref.1) | copy-start | bytes 1769476
  91.0 96.7 %copy-start.4 = (f32[64,18]{0,1:T(8,128)S(1)}, f32[64,18]{0,1:T(8,128)}, u32[]{:S(2)}) copy-start(f32[64,18]{0,1:T(8,128)} %param.17) | copy-start | bytes 13828
  91.0 97.4 %copy-start.5 = (f32[64,18]{0,1:T(8,128)S(1)}, f32[64,18]{0,1:T(8,128)}, u32[]{:S(2)}) copy-start(f32[64,18]{0,1:T(8,128)} %param.19) | copy-start | bytes 13828
  93.3 103.1 %copy-start = (bf16[256,2048]{1,0:T(8,128)(2,1)S(1)}, bf16[256,2048]{1,0:T(8,128)(2,1)}, u32[]{:S(2)}) copy-start(bf16[256,2048]{1,0:T(8,128)(2,1)} %shard_map.146) | copy-start | bytes 3145732
